TPU v7x, 32 devices: a whole 2x2x4 slice. The times are simulated.
32 devices in a mesh: slab: 8 (over z, core), grp: 4 (over y, x).
Axes of the slice: x: 2, y: 2, z: 4, core: 2. Of those that a mesh axis runs over, the one named last changes fastest.
Arguments:
- comp: float32 [256, 128, 128], P(('slab', 'grp')), may hold values from -1 to 1
- guess: float32 [64, 32, 32], P('slab', 'grp'), may hold values from -3 to 3
Outputs:
- comp_next: float32 [256, 128, 128], P(('slab', 'grp'))
- potential: float32 [64, 32, 32], P('slab', 'grp')
All inputs are finite; a program needn't handle non-finite values.
Results may differ from a plain program's by a relative error of at most 0.00002.
Values sent between devices are 32-bit elements; how exact they have to be, the bound alone decides.
No kernel may reach another device: no remote copies, remote signals or barrier semaphores. Data moves between devices by JAX's collectives and lax.ppermute only.
A program may use at most 64 MiB of HBM per device.

v0:
```python
import functools

import jax
import jax.numpy as jnp
from jax import lax
from jax.experimental import pallas as pl
from jax.experimental.pallas import tpu as pltpu
from jax.sharding import PartitionSpec as P

NCOARSE = 3
NPOST = 2

gradient_energy = 0.5
screening = 0.5
damping = 0.8
long_range = 4.0
time_step = 0.02

LANES = 128
QUAD = 4
HALO = 3

VMEM = pl.BlockSpec(memory_space=pltpu.VMEM)
PARAMS = pltpu.CompilerParams(vmem_limit_bytes=8 * 2**20)


def lanes_of(shape):
    return lax.broadcasted_iota(jnp.int32, shape, len(shape) - 1)


def rows_of(shape):
    return lax.broadcasted_iota(jnp.int32, shape, len(shape) - 2)


def exact_dot(a, b):
    return jnp.dot(a, b, preferred_element_type=jnp.float32, precision=lax.Precision.HIGHEST)


def pack_guess_kernel(guess_ref, packed_ref):
    planes, rows, columns = guess_ref.shape
    for quad in range(planes // QUAD):
        at = quad * rows
        for i in range(QUAD):
            packed_ref[at : at + rows, i * columns : (i + 1) * columns] = guess_ref[QUAD * quad + i]


def pack_guess(guess):
    return pl.pallas_call(
        pack_guess_kernel,
        out_shape=jax.ShapeDtypeStruct((16, LANES), jnp.float32),
        in_specs=[VMEM],
        out_specs=VMEM,
        cost_estimate=pl.CostEstimate(flops=10_000, bytes_accessed=40_000, transcendentals=0),
        compiler_params=PARAMS,
        name="pack_guess",
    )(guess)


def pack_kernel(comp_ref, guess_ref, message_ref, first_ref, second_ref):
    columns = 32
    rows = comp_ref.shape[1] // 4
    half = rows // 2
    message_ref[half:, :] = guess_ref[...]
    pooled = []
    for plane in range(comp_ref.shape[0] // 4):
        total = None
        for i in range(4):
            for j in range(4):
                part = comp_ref[4 * plane + i, pl.ds(j, rows, stride=4), :]
                total = part if total is None else total + part
        pooled.append(total)
    stacked = jnp.concatenate(
        [pooled[0][:half], pooled[1][:half], pooled[0][half:], pooled[1][half:]], axis=0
    )
    square = (comp_ref.shape[2], LANES)
    pool = jnp.where(rows_of(square) // 4 == lanes_of(square) % columns, 1.0 / 64.0, 0.0)
    spread = exact_dot(stacked, pool.astype(jnp.float32))
    where = lanes_of((half, LANES)) // columns
    packed = spread[:half]
    for block in range(1, QUAD):
        packed = jnp.where(where == block, spread[block * half : (block + 1) * half], packed)
    message_ref[0:half, :] = packed
    odd = lax.rem(lax.axis_index("grp"), 2)
    top = comp_ref.shape[0] - 2
    first_ref[...] = comp_ref[pl.ds(top * (1 - odd), 2)]
    second_ref[...] = comp_ref[pl.ds(top * odd, 2)]


def pack(comp, guess):
    outer = jax.ShapeDtypeStruct((2,) + comp.shape[1:], jnp.float32)
    message = jax.ShapeDtypeStruct((32, LANES), jnp.float32)
    return pl.pallas_call(
        pack_kernel,
        out_shape=(message, outer, outer),
        in_specs=[VMEM] * 2,
        out_specs=(VMEM,) * 3,
        cost_estimate=pl.CostEstimate(flops=2_000_000, bytes_accessed=800_000, transcendentals=0),
        compiler_params=PARAMS,
        name="pack",
    )(comp, pack_guess(guess))


def beside_in_plane(v):
    rows, lanes = rows_of(v.shape), lanes_of(v.shape)
    last_row, last_lane = v.shape[0] - 1, v.shape[1] - 1
    total = jnp.where(rows == 0, 0.0, pltpu.roll(v, 1, 0))
    total = total + jnp.where(rows == last_row, 0.0, pltpu.roll(v, last_row, 0))
    total = total + jnp.where(lanes == 0, 0.0, pltpu.roll(v, 1, 1))
    return total + jnp.where(lanes == last_lane, 0.0, pltpu.roll(v, last_lane, 1))


def base_kernel(comp_ref, first_ref, second_ref, base_ref, chem_ref):
    planes = comp_ref.shape[0]
    group, groups = lax.axis_index("grp"), lax.axis_size("grp")
    index = lax.axis_index("slab") * groups + group
    devices = lax.axis_size("slab") * groups
    odd = lax.rem(group, 2) == 1

    below = jnp.where(index > 0, 1.0, 0.0)
    above = jnp.where(index < devices - 1, 1.0, 0.0)

    def plane(f):
        if f < 0:
            return jnp.where(odd, first_ref[f + 2], second_ref[f + 2]) * below
        if f >= planes:
            return jnp.where(odd, second_ref[f - planes], first_ref[f - planes]) * above
        return comp_ref[f]

    for f in range(-1, planes + 1):
        c = plane(f)
        beside = beside_in_plane(c) + plane(f - 1) + plane(f + 1)
        chem = c * c * c - c - gradient_energy * (beside - 6.0 * c)
        if f < 0:
            chem = chem * below
        if f >= planes:
            chem = chem * above
        chem_ref[f + 1] = chem
    for f in range(planes):
        v = chem_ref[f + 1]
        beside = beside_in_plane(v) + chem_ref[f] + chem_ref[f + 2]
        base_ref[f] = comp_ref[f] + time_step * (beside - 6.0 * v)


def base_of(comp, first, second):
    return pl.pallas_call(
        base_kernel,
        out_shape=jax.ShapeDtypeStruct(comp.shape, jnp.float32),
        in_specs=[VMEM] * 3,
        out_specs=VMEM,
        scratch_shapes=[pltpu.VMEM((comp.shape[0] + 2,) + comp.shape[1:], jnp.float32)],
        cost_estimate=pl.CostEstimate(flops=6_000_000, bytes_accessed=1_500_000, transcendentals=0),
        compiler_params=PARAMS,
        name="base",
    )(comp, first, second)


def along(v, quad, step):
    shift = (-32 * step) % LANES
    here = pltpu.roll(v[quad], shift, 1)
    other = quad + (1 if step > 0 else -1)
    lanes = lanes_of(here.shape)
    own = lanes < LANES - 32 * step if step > 0 else lanes >= -32 * step
    if 0 <= other < len(v):
        return jnp.where(own, here, pltpu.roll(v[other], shift, 1))
    return jnp.where(own, here, 0.0)


def beside(v, quad, step):
    here = v[quad]
    rows, columns = rows_of(here.shape), lanes_of(here.shape) % 32
    total = along(v, quad, step) + along(v, quad, -step)
    total = total + jnp.where(rows < step, 0.0, pltpu.roll(here, step, 0))
    total = total + jnp.where(rows >= 32 - step, 0.0, pltpu.roll(here, 32 - step, 0))
    total = total + jnp.where(columns < step, 0.0, pltpu.roll(here, step, 1))
    return total + jnp.where(columns >= 32 - step, 0.0, pltpu.roll(here, LANES - step, 1))


def operated(v, quad):
    return screening * v[quad] - (beside(v, quad, 1) - 6.0 * v[quad])


def pair_sum(v, step, axis):
    index = (rows_of(v.shape), lanes_of(v.shape))[axis] // step
    other = v.shape[axis] - step
    return v + jnp.where(index % 2 == 0, pltpu.roll(v, other, axis), pltpu.roll(v, step, axis))


def square_sum(v):
    return pair_sum(pair_sum(v, 1, 1), 1, 0)


def cell_mean(v):
    return square_sum(pair_sum(v, 32, 1)) * 0.125


def in_plane(v):
    rows, columns = rows_of(v.shape), lanes_of(v.shape) % 32
    total = jnp.where(rows == 0, 0.0, pltpu.roll(v, 1, 0))
    total = total + jnp.where(rows == 31, 0.0, pltpu.roll(v, 31, 0))
    total = total + jnp.where(columns == 0, 0.0, pltpu.roll(v, 1, 1))
    return total + jnp.where(columns == 31, 0.0, pltpu.roll(v, LANES - 1, 1))


def source_of(even, uneven):
    low_half = lanes_of((16, LANES)) < 64
    top = jnp.where(low_half, even, pltpu.roll(uneven, 64, 1))
    bottom = jnp.where(low_half, pltpu.roll(even, 64, 1), uneven)
    return jnp.concatenate([top, bottom], axis=0)


def widen():
    square = (LANES, LANES)
    return jnp.where(rows_of(square) == lanes_of(square) // 4, 1.0, 0.0).astype(jnp.float32)


scale = damping / (screening + 6.0)
scale_b = damping / (screening + 1.5)
factor = time_step * long_range
edge_share = 0.125 * scale_b * (0.25 * scale_b) ** 2 * scale**2 * factor


def edge_kernel(own_ref, edge_ref, guess_s):
    groups, group = lax.axis_size("grp"), lax.axis_index("grp")
    quads, block = groups // 2, 32 // groups
    up = group == groups - 1
    at = 16 + jnp.where(up, (quads - 1) * block, 0)
    for g in range(groups):
        guess_s[g * block : (g + 1) * block] = own_ref[g, pl.ds(pl.multiple_of(at, block), block)]
    guess = guess_s[...]
    source = jnp.where(
        up,
        source_of(own_ref[groups - 2, 0:16], own_ref[groups - 1, 0:16]),
        source_of(own_ref[0, 0:16], own_ref[1, 0:16]),
    )
    inner = jnp.where(up, pltpu.roll(guess, 32, 1), pltpu.roll(guess, LANES - 32, 1))
    flat = in_plane(guess)
    pre = guess + scale * (source - (screening * guess - (flat + inner - 6.0 * guess)))
    value = square_sum(pre + scale * (flat - (screening + 5.0) * guess))
    value = jnp.where(up, pltpu.roll(value, 32, 1), value)
    edge_ref[...] = edge_share * exact_dot(value, widen())


def edge_of(own):
    return pl.pallas_call(
        edge_kernel,
        out_shape=jax.ShapeDtypeStruct((32, LANES), jnp.float32),
        in_specs=[VMEM],
        out_specs=VMEM,
        scratch_shapes=[pltpu.VMEM((32, LANES), jnp.float32)],
        cost_estimate=pl.CostEstimate(flops=500_000, bytes_accessed=80_000, transcendentals=0),
        compiler_params=PARAMS,
        name="edge",
    )(own)


def solve_kernel(edged, own_ref, core_ref, chip_ref, wide_ref, rows_ref, guess_s, window_s):
    groups = lax.axis_size("grp")
    slab, slabs, group = lax.axis_index("slab"), lax.axis_size("slab"), lax.axis_index("grp")
    quads = groups // 2
    block = 32 // groups
    odd = lax.rem(slab, 2) == 1

    def low(*at):
        return jnp.where(odd, core_ref[at], chip_ref[at])

    def high(*at):
        return jnp.where(odd, chip_ref[at], core_ref[at])

    def own(*at):
        return own_ref[at]

    source = []

    def take(read, quad):
        at = len(source)
        source.append(source_of(read(2 * quad, pl.ds(0, 16)), read(2 * quad + 1, pl.ds(0, 16))))
        for g in range(groups):
            guess_s[at, g * block : (g + 1) * block] = read(g, pl.ds(16 + quad * block, block))

    near, trim = (quads, 0) if edged else (HALO, 1)
    for quad in range(quads - near, quads):
        take(low, quad)
    for quad in range(quads):
        take(own, quad)
    for quad in range(near):
        take(high, quad)
    total = quads + 2 * near
    has_low = jnp.where(slab > 0, 1.0, 0.0)
    has_high = jnp.where(slab < slabs - 1, 1.0, 0.0)

    def kept(v, quad):
        if quad < near:
            return v * has_low
        return v if quad < near + quads else v * has_high

    guess = [kept(guess_s[quad], quad) for quad in range(total)]
    pre = [
        kept(guess[quad] + scale * (source[quad] - operated(guess, quad)), quad)
        for quad in range(total)
    ]
    coarsest = [
        kept(cell_mean(source[quad] - operated(pre, quad)), quad)
        for quad in range(trim, total - trim)
    ]
    correction = [scale_b * v for v in coarsest]
    for sweep in range(NCOARSE - 1):
        last = sweep == NCOARSE - 2
        updated = []
        for quad in range(len(correction)):
            if last and quad in (0, len(correction) - 1):
                updated.append(None)
                continue
            c = correction[quad]
            applied = screening * c - 0.25 * (beside(correction, quad, 2) - 6.0 * c)
            updated.append(kept(c + scale_b * (coarsest[quad] - applied), quad + trim))
        correction = updated
    start = near - 1
    found = [pre[quad] + correction[quad - trim] for quad in range(start, total - start)]
    for _ in range(NPOST):
        found = [
            kept(v + scale * (source[quad + start] - operated(found, quad)), quad + start)
            for quad, v in enumerate(found)
        ]

    for quad in range(len(found)):
        window_s[quad] = found[quad]
    for quad in range(quads):
        rows_ref[quad] = window_s[quad + 1, pl.ds(pl.multiple_of(group * block, block), block), :]

    picked = []
    for i in range(4):
        at = 2 * group + 3 + i
        picked.append(
            pltpu.roll(window_s[at // QUAD], lax.rem(LANES - 32 * lax.rem(at, QUAD), LANES), 1)
        )
    if edged:
        lowest = group == 0
        facing = jnp.where(lowest, guess[0], pltpu.roll(guess[total - 1], 32, 1))
        reach = jnp.where(lowest, slab, slabs - 1 - slab) >= 2
        picked.append(jnp.where(reach, edge_share * scale / factor, 0.0) * square_sum(facing))
    wide = factor * exact_dot(jnp.concatenate(picked, axis=0), widen())
    wide = [wide[32 * i : 32 * (i + 1)] for i in range(len(picked))]
    if edged:
        wide[0] = wide[0] + jnp.where(group == 0, 1.0, 0.0) * wide[4]
        wide[3] = wide[3] + jnp.where(group == groups - 1, 1.0, 0.0) * wide[4]
    for i in range(4):
        wide_ref[i] = wide[i]


def solve(own, core, chip, guess, edged):
    groups = own.shape[0]
    quads = groups // 2
    total = 3 * quads if edged else quads + 2 * HALO
    return pl.pallas_call(
        functools.partial(solve_kernel, edged),
        out_shape=(
            jax.ShapeDtypeStruct((4, 32, LANES), jnp.float32),
            jax.ShapeDtypeStruct((quads, guess.shape[1], LANES), jnp.float32),
        ),
        in_specs=[VMEM] * 3,
        out_specs=(VMEM, VMEM),
        scratch_shapes=[
            pltpu.VMEM((total, 32, LANES), jnp.float32),
            pltpu.VMEM((quads + 2, 32, LANES), jnp.float32),
        ],
        cost_estimate=pl.CostEstimate(flops=6_000_000, bytes_accessed=500_000, transcendentals=0),
        compiler_params=PARAMS,
        name="solve",
    )(own, core, chip)


def finish_kernel(base_ref, wide_ref, rows_ref, *refs):
    edge_ref = refs[0] if len(refs) == 3 else None
    next_ref, potential_ref = refs[-2:]
    group, groups = lax.axis_index("grp"), lax.axis_size("grp")
    slab, slabs = lax.axis_index("slab"), lax.axis_size("slab")
    for quad in range(rows_ref.shape[0]):
        for i in range(QUAD):
            potential_ref[QUAD * quad + i] = rows_ref[quad, :, 32 * i : 32 * (i + 1)]
    wide = [wide_ref[i] for i in range(4)]
    if edge_ref is not None:
        lowest = (group == 0) & (slab >= 2)
        highest = (group == groups - 1) & (slab < slabs - 2)
        wide[0] = wide[0] + jnp.where(lowest, 1.0, 0.0) * edge_ref[...]
        wide[3] = wide[3] + jnp.where(highest, 1.0, 0.0) * edge_ref[...]
    rows, lanes = rows_of((32, LANES)), lanes_of((32, LANES))
    for coarse in range(2):
        here = wide[coarse + 1]
        across = jnp.where(lanes == 0, 0.0, pltpu.roll(here, 1, 1))
        across = across + jnp.where(lanes == LANES - 1, 0.0, pltpu.roll(here, LANES - 1, 1))
        middle = across - 2.0 * here
        before = middle + (jnp.where(rows == 0, 0.0, pltpu.roll(here, 1, 0)) - here)
        after = middle + (jnp.where(rows == 31, 0.0, pltpu.roll(here, 31, 0)) - here)
        down = wide[coarse] - here
        up = wide[coarse + 2] - here
        for f in range(4):
            for j in range(4):
                term = (before, middle, middle, after)[j]
                if f == 0:
                    term = term + down
                if f == 3:
                    term = term + up
                at = (4 * coarse + f, pl.ds(j, 32, stride=4), slice(None))
                next_ref[at] = base_ref[at] + term


def finish(base, wide, rows, edge, guess):
    operands = [base, wide, rows] + ([] if edge is None else [edge])
    return pl.pallas_call(
        finish_kernel,
        out_shape=(
            jax.ShapeDtypeStruct(base.shape, jnp.float32),
            jax.ShapeDtypeStruct(guess.shape, jnp.float32),
        ),
        in_specs=[VMEM] * len(operands),
        out_specs=(VMEM, VMEM),
        cost_estimate=pl.CostEstimate(flops=500_000, bytes_accessed=1_100_000, transcendentals=0),
        compiler_params=PARAMS,
        name="finish",
    )(*operands)


def pairing(*pairs):
    return [p for a, b in pairs for p in {(a, b), (b, a)}]


def per_device(comp, guess):
    slabs, groups = lax.axis_size("slab"), lax.axis_size("grp")
    group = lax.axis_index("grp")
    both = ("slab", "grp")
    devices = slabs * groups
    quads = groups // 2

    def at(slab, member):
        return slab * groups + member

    message, first, second = pack(comp, guess)


    bundle = jnp.zeros((groups,) + message.shape, jnp.float32)
    bundle = lax.dynamic_update_slice(bundle, message[None], (group, 0, 0))
    for k in range(1, groups):
        block = lax.ppermute(message, "grp", [(i, i ^ k) for i in range(groups)])
        bundle = lax.dynamic_update_slice(bundle, block[None], (group ^ k, 0, 0))

    first = lax.ppermute(first, both, pairing(*((d, d + 1) for d in range(0, devices, 2))))
    second = lax.ppermute(
        second,
        both,
        pairing(
            *((d, d + 1) for d in range(1, devices - 1, 2)), *idle_second(devices)
        ),
    )

    core = lax.ppermute(bundle, "slab", pairing(*((i, i + 1) for i in range(0, slabs, 2))))
    chip = lax.ppermute(
        bundle,
        both,
        pairing(
            *((at(i, g), at(i + 1, g)) for i in range(1, slabs - 1, 2) for g in range(groups)),
            *idle_chip(at, slabs, groups),
        ),
    )
    edge = None
    if quads < HALO:
        edge = lax.ppermute(edge_of(bundle), both, edge_pairs(at, slabs, groups))

    base = base_of(comp, first, second)
    wide, rows = solve(bundle, core, chip, guess, edge is not None)
    return finish(base, wide, rows, edge, guess)


def idle_second(devices):
    return [(0, 0), (devices - 1, devices - 1)]


def idle_chip(at, slabs, groups):
    half = groups // 2
    return [(at(s, g), at(s, g + half)) for s in (0, slabs - 1) for g in range(half)]


def edge_pairs(at, slabs, groups):
    top = groups - 1
    return pairing(
        *((at(i, top), at(i + 2, 0)) for i in range(slabs - 2)),
        *((at(i, g), at(i + 1, g)) for i in range(0, slabs, 2) for g in range(1, top)),
        (at(0, 0), at(1, 0)),
        (at(slabs - 2, top), at(slabs - 1, top)),
    )


def solution(mesh):
    placed = (P(("slab", "grp"), None, None), P("slab", "grp", None))
    return jax.shard_map(per_device, mesh=mesh, in_specs=placed, out_specs=placed, check_vma=False)
```

profile of v0, /device:TPU:0, one launch (start us, length us, event | category | flops | bytes accessed | tf_op | source)
XLA Modules:
  0.0 19.3 jit_solution(3737989776917139048)
XLA Ops:
  0.6 0.0 copy-start.2
  0.6 0.7 %copy-done.2 = f32[8,8,32]{2,1,0:T(8,128)S(1)} copy-done((f32[8,8,32]{2,1,0:T(8,128)S(1)}, f32[8,8,32]{2,1,0:T(8,128)}, u32[]{:S(2)}) %copy-start.2) | copy-done | bytes 8216
  1.4 0.1 pack_guess.1.guess_ref
  1.5 0.0 copy-start
  1.5 1.0 %copy-done = f32[8,128,128]{2,1,0:T(8,128)S(1)} copy-done((f32[8,128,128]{2,1,0:T(8,128)S(1)}, f32[8,128,128]{2,1,0:T(8,128)}, u32[]{:S(2)}) %copy-start) | copy-done | bytes 524312
  2.5 0.0 copy-start.1
  2.5 0.2 pack.1
  2.7 4.0 %collective-permute-start.4 = (f32[32,128]{1,0:T(8,128)S(1)}, f32[32,128]{1,0:T(8,128)S(1)}, u32[]{:S(2)}, u32[]{:S(2)}) collective-permute-start(f32[32,128]{1,0:T(8,128)S(1)} %get-tuple-element.9), channel_id=1, source_target_pairs={{0,3},{1,2},{2,1},{3,0},{4,7},{5,6},{6,5},{7,4},{8,11},{9,10},{10,... | collective-permute-start | bytes 49160 | tf_op jit(solution)/shard_map/ppermute | solution.py:443
  6.7 0.5 %collective-permute-start.3 = (f32[32,128]{1,0:T(8,128)S(1)}, f32[32,128]{1,0:T(8,128)S(1)}, u32[]{:S(2)}, u32[]{:S(2)}) collective-permute-start(f32[32,128]{1,0:T(8,128)S(1)} %get-tuple-element.9), channel_id=1, source_target_pairs={{0,2},{1,3},{2,0},{3,1},{4,6},{5,7},{6,4},{7,5},{8,10},{9,11},{10,... | collective-permute-start | bytes 49160 | tf_op jit(solution)/shard_map/ppermute | solution.py:443
  7.2 0.1 collective-permute-start.2
  7.3 1.9 %collective-permute-start = (f32[2,128,128]{2,1,0:T(8,128)S(1)}, f32[2,128,128]{2,1,0:T(8,128)S(1)}, u32[]{:S(2)}, u32[]{:S(2)}) collective-permute-start(f32[2,128,128]{2,1,0:T(8,128)S(1)} %get-tuple-element.7), channel_id=1, source_target_pairs={{0,1},{1,0},{2,3},{3,2},{4,5},{5,4},{6,7},{7,6},{8,9},{9,8},{10,11... | collective-permute-start | bytes 393224 | tf_op jit(solution)/shard_map/ppermute | solution.py:446
  9.2 0.7 %collective-permute-start.1 = (f32[2,128,128]{2,1,0:T(8,128)S(1)}, f32[2,128,128]{2,1,0:T(8,128)S(1)}, u32[]{:S(2)}, u32[]{:S(2)}) collective-permute-start(f32[2,128,128]{2,1,0:T(8,128)S(1)} %get-tuple-element.8), channel_id=1, source_target_pairs={{1,2},{2,1},{3,4},{4,3},{5,6},{6,5},{8,7},{7,8},{9,10},{10,9},{11,... | collective-permute-start | bytes 393224 | tf_op jit(solution)/shard_map/ppermute | solution.py:447
  9.9 1.0 %collective-permute-done.2 = f32[32,128]{1,0:T(8,128)S(1)} collective-permute-done((f32[32,128]{1,0:T(8,128)S(1)}, f32[32,128]{1,0:T(8,128)S(1)}, u32[]{:S(2)}, u32[]{:S(2)}) %collective-permute-start.2) | collective-permute-done | bytes 16416 | tf_op jit(solution)/shard_map/ppermute | solution.py:443
  10.9 0.0 collective-permute-done.3
  11.0 0.0 collective-permute-done.4
  11.0 1.9 %collective-permute-start.6 = (f32[4,32,128]{2,1,0:T(8,128)S(1)}, f32[4,32,128]{2,1,0:T(8,128)S(1)}, u32[]{:S(2)}, u32[]{:S(2)}) collective-permute-start(f32[4,32,128]{2,1,0:T(8,128)S(1)} %bitcast_dynamic-update-slice_fusion.own_ref), channel_id=1, source_target_pairs={{8,4},{4,8},{5,9},{9,5},{10,6},{6,10},{11,7},{7,11},{12,16},{16,12... | collective-permute-start | bytes 196616 | tf_op jit(solution)/shard_map/ppermute | solution.py:456
  12.9 0.1 collective-permute-start.5
  13.0 0.4 %edge.1 = f32[32,128]{1,0:T(8,128)S(1)} custom-call(f32[4,32,128]{2,1,0:T(8,128)S(1)} %bitcast_dynamic-update-slice_fusion.own_ref), custom_call_target="tpu_custom_call" | custom-call | flops 500000 | bytes 80000 | tf_op jit(solution)/shard_map/edge/pallas_call | solution.py:244
  13.4 0.4 %collective-permute-start.7 = (f32[32,128]{1,0:T(8,128)S(1)}, f32[32,128]{1,0:T(8,128)S(1)}, u32[]{:S(2)}, u32[]{:S(2)}) collective-permute-start(f32[32,128]{1,0:T(8,128)S(1)} %edge.1), channel_id=1, source_target_pairs={{3,8},{8,3},{12,7},{7,12},{16,11},{11,16},{20,15},{15,20},{19,24},... | collective-permute-start | bytes 49160 | tf_op jit(solution)/shard_map/ppermute | solution.py:466
  13.8 2.4 %collective-permute-done.6.chip_ref = f32[4,32,128]{2,1,0:T(8,128)S(1)} collective-permute-done((f32[4,32,128]{2,1,0:T(8,128)S(1)}, f32[4,32,128]{2,1,0:T(8,128)S(1)}, u32[]{:S(2)}, u32[]{:S(2)}) %collective-permute-start.6) | collective-permute-done | bytes 65568 | tf_op jit(solution)/shard_map/ppermute | solution.py:456
  16.3 0.0 collective-permute-done.5.core_ref
  16.3 1.4 %solve.1 = (f32[4,32,128]{2,1,0:T(8,128)S(1)}, f32[2,8,128]{2,1,0:T(8,128)S(1)}) custom-call(f32[4,32,128]{2,1,0:T(8,128)S(1)} %bitcast_dynamic-update-slice_fusion.own_ref, f32[4,32,128]{2,1,0:T(8,128)S(1)} %collective-permute-done.5.core_ref, f32[4,32,128]{2,1,0:T(8,128)S(1)} %collective-permute-done.6.chip_ref), custom_call_target="tpu_custom_call" | custom-call | flops 6000000 | bytes 500000 | tf_op jit(solution)/shard_map/solve/pallas_call | solution.py:354
  17.6 0.0 collective-permute-done.first_ref
  17.6 0.0 collective-permute-done.1.second_ref
  17.6 0.0 copy-done.1
  17.7 0.7 %base.1.base_ref = f32[8,128,128]{2,1,0:T(8,128)S(1)} custom-call(f32[8,128,128]{2,1,0:T(8,128)S(1)} %copy-done.1, f32[2,128,128]{2,1,0:T(8,128)S(1)} %collective-permute-done.first_ref, f32[2,128,128]{2,1,0:T(8,128)S(1)} %collective-permute-done.1.second_ref), custom_call_target="tpu_custom_call" | custom-call | flops 6000000 | bytes 1500000 | tf_op jit(solution)/shard_map/base/pallas_call | solution.py:145
  18.4 0.0 collective-permute-done.7.refs_0_
  18.4 0.9 %finish.1 = (f32[8,128,128]{2,1,0:T(8,128)}, f32[8,8,32]{2,1,0:T(8,128)}) custom-call(f32[8,128,128]{2,1,0:T(8,128)S(1)} %base.1.base_ref, f32[4,32,128]{2,1,0:T(8,128)S(1)} %get-tuple-element.10.wide_ref, f32[2,8,128]{2,1,0:T(8,128)S(1)} %get-tuple-element.11.rows_ref, f32[32,128]{1,0:T(8,128)S(1)} %collective-permute-done.7.refs_0_), custom_call_target="tpu_custom_call" | custom-call | flops 500000 | bytes 1100000 | tf_op jit(solution)/shard_map/finish/pallas_call | solution.py:409
  (5 shorter events, 0.0 us)
Async XLA Ops:
  0.6 0.8 %copy-start.2 = (f32[8,8,32]{2,1,0:T(8,128)S(1)}, f32[8,8,32]{2,1,0:T(8,128)}, u32[]{:S(2)}) copy-start(f32[8,8,32]{2,1,0:T(8,128)} %guess_ref.1) | copy-start | bytes 24580
  1.5 1.0 %copy-start = (f32[8,128,128]{2,1,0:T(8,128)S(1)}, f32[8,128,128]{2,1,0:T(8,128)}, u32[]{:S(2)}) copy-start(f32[8,128,128]{2,1,0:T(8,128)} %comp_ref.3) | copy-start | bytes 1572868
  2.5 15.1 %copy-start.1 = (f32[8,128,128]{2,1,0:T(8,128)S(1)}, f32[8,128,128]{2,1,0:T(8,128)}, u32[]{:S(2)}) copy-start(f32[8,128,128]{2,1,0:T(8,128)} %comp_ref.3) | copy-start | bytes 1572868
  2.7 8.3 %collective-permute-start.4 = (f32[32,128]{1,0:T(8,128)S(1)}, f32[32,128]{1,0:T(8,128)S(1)}, u32[]{:S(2)}, u32[]{:S(2)}) collective-permute-start(f32[32,128]{1,0:T(8,128)S(1)} %get-tuple-element.9), channel_id=1, source_target_pairs={{0,3},{1,2},{2,1},{3,0},{4,7},{5,6},{6,5},{7,4},{8,11},{9,10},{10,... | collective-permute-start | bytes 49160 | tf_op jit(solution)/shard_map/ppermute | solution.py:443
  6.7 4.3 %collective-permute-start.3 = (f32[32,128]{1,0:T(8,128)S(1)}, f32[32,128]{1,0:T(8,128)S(1)}, u32[]{:S(2)}, u32[]{:S(2)}) collective-permute-start(f32[32,128]{1,0:T(8,128)S(1)} %get-tuple-element.9), channel_id=1, source_target_pairs={{0,2},{1,3},{2,0},{3,1},{4,6},{5,7},{6,4},{7,5},{8,10},{9,11},{10,... | collective-permute-start | bytes 49160 | tf_op jit(solution)/shard_map/ppermute | solution.py:443
  7.2 3.7 %collective-permute-start.2 = (f32[32,128]{1,0:T(8,128)S(1)}, f32[32,128]{1,0:T(8,128)S(1)}, u32[]{:S(2)}, u32[]{:S(2)}) collective-permute-start(f32[32,128]{1,0:T(8,128)S(1)} %get-tuple-element.9), channel_id=1, source_target_pairs={{0,1},{1,0},{2,3},{3,2},{4,5},{5,4},{6,7},{7,6},{8,9},{9,8},{10,11... | collective-permute-start | bytes 49160 | tf_op jit(solution)/shard_map/ppermute | solution.py:443
  7.3 10.3 %collective-permute-start = (f32[2,128,128]{2,1,0:T(8,128)S(1)}, f32[2,128,128]{2,1,0:T(8,128)S(1)}, u32[]{:S(2)}, u32[]{:S(2)}) collective-permute-start(f32[2,128,128]{2,1,0:T(8,128)S(1)} %get-tuple-element.7), channel_id=1, source_target_pairs={{0,1},{1,0},{2,3},{3,2},{4,5},{5,4},{6,7},{7,6},{8,9},{9,8},{10,11... | collective-permute-start | bytes 393224 | tf_op jit(solution)/shard_map/ppermute | solution.py:446
  9.2 8.4 %collective-permute-start.1 = (f32[2,128,128]{2,1,0:T(8,128)S(1)}, f32[2,128,128]{2,1,0:T(8,128)S(1)}, u32[]{:S(2)}, u32[]{:S(2)}) collective-permute-start(f32[2,128,128]{2,1,0:T(8,128)S(1)} %get-tuple-element.8), channel_id=1, source_target_pairs={{1,2},{2,1},{3,4},{4,3},{5,6},{6,5},{8,7},{7,8},{9,10},{10,9},{11,... | collective-permute-start | bytes 393224 | tf_op jit(solution)/shard_map/ppermute | solution.py:447
  11.0 5.3 %collective-permute-start.6 = (f32[4,32,128]{2,1,0:T(8,128)S(1)}, f32[4,32,128]{2,1,0:T(8,128)S(1)}, u32[]{:S(2)}, u32[]{:S(2)}) collective-permute-start(f32[4,32,128]{2,1,0:T(8,128)S(1)} %bitcast_dynamic-update-slice_fusion.own_ref), channel_id=1, source_target_pairs={{8,4},{4,8},{5,9},{9,5},{10,6},{6,10},{11,7},{7,11},{12,16},{16,12... | collective-permute-start | bytes 196616 | tf_op jit(solution)/shard_map/ppermute | solution.py:456
  12.9 3.3 %collective-permute-start.5 = (f32[4,32,128]{2,1,0:T(8,128)S(1)}, f32[4,32,128]{2,1,0:T(8,128)S(1)}, u32[]{:S(2)}, u32[]{:S(2)}) collective-permute-start(f32[4,32,128]{2,1,0:T(8,128)S(1)} %bitcast_dynamic-update-slice_fusion.own_ref), channel_id=1, source_target_pairs={{0,4},{4,0},{8,12},{12,8},{16,20},{20,16},{24,28},{28,24},{1,5},{5... | collective-permute-start | bytes 196616 | tf_op jit(solution)/shard_map/ppermute | solution.py:455
  13.4 5.0 %collective-permute-start.7 = (f32[32,128]{1,0:T(8,128)S(1)}, f32[32,128]{1,0:T(8,128)S(1)}, u32[]{:S(2)}, u32[]{:S(2)}) collective-permute-start(f32[32,128]{1,0:T(8,128)S(1)} %edge.1), channel_id=1, source_target_pairs={{3,8},{8,3},{12,7},{7,12},{16,11},{11,16},{20,15},{15,20},{19,24},... | collective-permute-start | bytes 49160 | tf_op jit(solution)/shard_map/ppermute | solution.py:466
where the time goes:
time: 19.6 us; the launch traced here: 19.3 us
  starting transfers between devices  9.64 us (49%)
  Pallas kernels  3.68 us (19%)
  waiting for transfers between devices  3.43 us (18%)
  local copies, waits for them, and re-layouts  1.83 us (9%)
  between operations  0.76 us (4%)
    ppermute x3, starting transfers between devices, per_device(): block = lax.ppermute(message, 'grp', [(i, i ^ k) for i in range(groups)])  4.63 us
    ppermute x1, waiting for transfers between devices, per_device(): lax.ppermute(bundle, both, pairing(*((at(i, g), at(i + 1, g)) for i in ra...  2.42 us
    ppermute x1, starting transfers between devices, per_device(): lax.ppermute(bundle, both, pairing(*((at(i, g), at(i + 1, g)) for i in ra...  1.94 us
    ppermute x1, starting transfers between devices, per_device(): lax.ppermute(first, both, pairing(*((d, d + 1) for d in range(0, devices,...  1.89 us
    unnamed x6, local copies, waits for them, and re-layouts  1.8 us
    pallas_call x1, Pallas kernels, solve(): pl.pallas_call(functools.partial(solve_kernel, edged), out_shape=(jax.Sha...  1.36 us
    ppermute x3, waiting for transfers between devices, per_device(): block = lax.ppermute(message, 'grp', [(i, i ^ k) for i in range(groups)])  1 us
    pallas_call x1, Pallas kernels, finish(): pl.pallas_call(finish_kernel, out_shape=(jax.ShapeDtypeStruct(base.shape,...  0.92 us
  transfers between devices with their start and end apart: 8, of which 2 were waited for; matrix products, arithmetic and copies ran while one was open for 0% of the time, Pallas kernels for 13%

commit v1 on v0

--- a/solution.py
+++ b/solution.py
@@ -20,6 +20,8 @@
 QUAD = 4
 HALO = 3
 
+POOL_FLOPS = 300_000_000
+
 VMEM = pl.BlockSpec(memory_space=pltpu.VMEM)
 PARAMS = pltpu.CompilerParams(vmem_limit_bytes=8 * 2**20)
 
@@ -36,31 +38,10 @@
     return jnp.dot(a, b, preferred_element_type=jnp.float32, precision=lax.Precision.HIGHEST)
 
 
-def pack_guess_kernel(guess_ref, packed_ref):
-    planes, rows, columns = guess_ref.shape
-    for quad in range(planes // QUAD):
-        at = quad * rows
-        for i in range(QUAD):
-            packed_ref[at : at + rows, i * columns : (i + 1) * columns] = guess_ref[QUAD * quad + i]
-
-
-def pack_guess(guess):
-    return pl.pallas_call(
-        pack_guess_kernel,
-        out_shape=jax.ShapeDtypeStruct((16, LANES), jnp.float32),
-        in_specs=[VMEM],
-        out_specs=VMEM,
-        cost_estimate=pl.CostEstimate(flops=10_000, bytes_accessed=40_000, transcendentals=0),
-        compiler_params=PARAMS,
-        name="pack_guess",
-    )(guess)
-
-
-def pack_kernel(comp_ref, guess_ref, message_ref, first_ref, second_ref):
+def pool_kernel(comp_ref, source_ref, first_ref, second_ref):
     columns = 32
     rows = comp_ref.shape[1] // 4
     half = rows // 2
-    message_ref[half:, :] = guess_ref[...]
     pooled = []
     for plane in range(comp_ref.shape[0] // 4):
         total = None
@@ -79,25 +60,45 @@
     packed = spread[:half]
     for block in range(1, QUAD):
         packed = jnp.where(where == block, spread[block * half : (block + 1) * half], packed)
-    message_ref[0:half, :] = packed
+    source_ref[...] = packed
     odd = lax.rem(lax.axis_index("grp"), 2)
     top = comp_ref.shape[0] - 2
     first_ref[...] = comp_ref[pl.ds(top * (1 - odd), 2)]
     second_ref[...] = comp_ref[pl.ds(top * odd, 2)]
 
 
+def pack_kernel(source_ref, guess_ref, message_ref):
+    message_ref[0:16, :] = source_ref[...]
+    planes, rows, columns = guess_ref.shape
+    for quad in range(planes // QUAD):
+        at = 16 + quad * rows
+        for i in range(QUAD):
+            message_ref[at : at + rows, i * columns : (i + 1) * columns] = guess_ref[QUAD * quad + i]
+
+
 def pack(comp, guess):
     outer = jax.ShapeDtypeStruct((2,) + comp.shape[1:], jnp.float32)
-    message = jax.ShapeDtypeStruct((32, LANES), jnp.float32)
-    return pl.pallas_call(
+    source, first, second = pl.pallas_call(
+        pool_kernel,
+        out_shape=(jax.ShapeDtypeStruct((16, LANES), jnp.float32), outer, outer),
+        in_specs=[VMEM],
+        out_specs=(VMEM,) * 3,
+        cost_estimate=pl.CostEstimate(
+            flops=POOL_FLOPS, bytes_accessed=800_000, transcendentals=0
+        ),
+        compiler_params=PARAMS,
+        name="pool",
+    )(comp)
+    message = pl.pallas_call(
         pack_kernel,
-        out_shape=(message, outer, outer),
+        out_shape=jax.ShapeDtypeStruct((32, LANES), jnp.float32),
         in_specs=[VMEM] * 2,
-        out_specs=(VMEM,) * 3,
-        cost_estimate=pl.CostEstimate(flops=2_000_000, bytes_accessed=800_000, transcendentals=0),
+        out_specs=VMEM,
+        cost_estimate=pl.CostEstimate(flops=10_000, bytes_accessed=40_000, transcendentals=0),
         compiler_params=PARAMS,
         name="pack",
-    )(comp, pack_guess(guess))
+    )(source, guess)
+    return message, first, second
 
 
 def beside_in_plane(v):
@@ -109,74 +110,97 @@
     return total + jnp.where(lanes == last_lane, 0.0, pltpu.roll(v, last_lane, 1))
 
 
-def base_kernel(comp_ref, first_ref, second_ref, base_ref, chem_ref):
+def chem_of(below, c, above):
+    beside = beside_in_plane(c) + below + above
+    return c * c * c - c - gradient_energy * (beside - 6.0 * c)
+
+
+def stepped(c, below, v, above):
+    beside = beside_in_plane(v) + below + above
+    return c + time_step * (beside - 6.0 * v)
+
+
+def inner_kernel(comp_ref, base_ref, chem_ref):
+    planes = comp_ref.shape[0]
+    for f in range(1, planes - 1):
+        chem_ref[f] = chem_of(comp_ref[f - 1], comp_ref[f], comp_ref[f + 1])
+    for f in range(2, planes - 2):
+        base_ref[f] = stepped(comp_ref[f], chem_ref[f - 1], chem_ref[f], chem_ref[f + 1])
+
+
+def inner_of(comp):
+    shape = jax.ShapeDtypeStruct(comp.shape, jnp.float32)
+    return pl.pallas_call(
+        inner_kernel,
+        out_shape=(shape, shape),
+        in_specs=[VMEM],
+        out_specs=(VMEM, VMEM),
+        cost_estimate=pl.CostEstimate(flops=3_000_000, bytes_accessed=1_500_000, transcendentals=0),
+        compiler_params=PARAMS,
+        name="inner",
+    )(comp)
+
+
+def outer_kernel(comp_ref, first_ref, second_ref, chem_ref, base_ref):
     planes = comp_ref.shape[0]
     group, groups = lax.axis_index("grp"), lax.axis_size("grp")
     index = lax.axis_index("slab") * groups + group
     devices = lax.axis_size("slab") * groups
     odd = lax.rem(group, 2) == 1
-
     below = jnp.where(index > 0, 1.0, 0.0)
     above = jnp.where(index < devices - 1, 1.0, 0.0)
-
-    def plane(f):
-        if f < 0:
-            return jnp.where(odd, first_ref[f + 2], second_ref[f + 2]) * below
-        if f >= planes:
-            return jnp.where(odd, second_ref[f - planes], first_ref[f - planes]) * above
-        return comp_ref[f]
-
-    for f in range(-1, planes + 1):
-        c = plane(f)
-        beside = beside_in_plane(c) + plane(f - 1) + plane(f + 1)
-        chem = c * c * c - c - gradient_energy * (beside - 6.0 * c)
-        if f < 0:
-            chem = chem * below
-        if f >= planes:
-            chem = chem * above
-        chem_ref[f + 1] = chem
-    for f in range(planes):
-        v = chem_ref[f + 1]
-        beside = beside_in_plane(v) + chem_ref[f] + chem_ref[f + 2]
-        base_ref[f] = comp_ref[f] + time_step * (beside - 6.0 * v)
-
-
-def base_of(comp, first, second):
+    sides = (
+        (0, 1, 2, below, first_ref, second_ref, 1, 0),
+        (planes - 1, planes - 2, planes - 3, above, second_ref, first_ref, 0, 1),
+    )
+    for side, (edge, next_in, third, there, if_odd, if_even, near, far) in enumerate(sides):
+        c, inner = comp_ref[edge], comp_ref[next_in]
+        beyond = jnp.where(odd, if_odd[near], if_even[near]) * there
+        further = jnp.where(odd, if_odd[far], if_even[far]) * there
+        chem_beyond = chem_of(further, beyond, c) * there
+        chem_edge = chem_of(beyond, c, inner)
+        base_ref[3 * side] = stepped(c, chem_beyond, chem_edge, chem_ref[next_in])
+        base_ref[1 + side] = stepped(inner, chem_edge, chem_ref[next_in], chem_ref[third])
+
+
+def outer_of(comp, first, second, chem):
     return pl.pallas_call(
-        base_kernel,
-        out_shape=jax.ShapeDtypeStruct(comp.shape, jnp.float32),
-        in_specs=[VMEM] * 3,
+        outer_kernel,
+        out_shape=jax.ShapeDtypeStruct((4,) + comp.shape[1:], jnp.float32),
+        in_specs=[VMEM] * 4,
         out_specs=VMEM,
-        scratch_shapes=[pltpu.VMEM((comp.shape[0] + 2,) + comp.shape[1:], jnp.float32)],
-        cost_estimate=pl.CostEstimate(flops=6_000_000, bytes_accessed=1_500_000, transcendentals=0),
-        compiler_params=PARAMS,
-        name="base",
-    )(comp, first, second)
-
-
-def along(v, quad, step):
-    shift = (-32 * step) % LANES
-    here = pltpu.roll(v[quad], shift, 1)
-    other = quad + (1 if step > 0 else -1)
-    lanes = lanes_of(here.shape)
-    own = lanes < LANES - 32 * step if step > 0 else lanes >= -32 * step
-    if 0 <= other < len(v):
-        return jnp.where(own, here, pltpu.roll(v[other], shift, 1))
-    return jnp.where(own, here, 0.0)
-
-
-def beside(v, quad, step):
+        cost_estimate=pl.CostEstimate(flops=3_000_000, bytes_accessed=1_500_000, transcendentals=0),
+        compiler_params=PARAMS,
+        name="outer",
+    )(comp, first, second, chem)
+
+
+def rolled(v, step):
+    on = [pltpu.roll(here, LANES - 32 * step, 1) for here in v]
+    back = on if 64 * step == LANES else [pltpu.roll(here, 32 * step, 1) for here in v]
+    return on, back
+
+
+def beside(v, quad, step, turned):
     here = v[quad]
-    rows, columns = rows_of(here.shape), lanes_of(here.shape) % 32
-    total = along(v, quad, step) + along(v, quad, -step)
+    on, back = turned
+    rows, lanes = rows_of(here.shape), lanes_of(here.shape)
+    columns = lanes % 32
+    next_quad = on[quad + 1] if quad + 1 < len(v) else 0.0
+    last_quad = back[quad - 1] if quad else 0.0
+    total = jnp.where(lanes < LANES - 32 * step, on[quad], next_quad)
+    total = total + jnp.where(lanes >= 32 * step, back[quad], last_quad)
     total = total + jnp.where(rows < step, 0.0, pltpu.roll(here, step, 0))
     total = total + jnp.where(rows >= 32 - step, 0.0, pltpu.roll(here, 32 - step, 0))
     total = total + jnp.where(columns < step, 0.0, pltpu.roll(here, step, 1))
     return total + jnp.where(columns >= 32 - step, 0.0, pltpu.roll(here, LANES - step, 1))
 
 
-def operated(v, quad):
-    return screening * v[quad] - (beside(v, quad, 1) - 6.0 * v[quad])
+def operated(v):
+    turned = rolled(v, 1)
+    return [
+        screening * here - (beside(v, quad, 1, turned) - 6.0 * here) for quad, here in enumerate(v)
+    ]
 
 
 def pair_sum(v, step, axis):
@@ -294,31 +318,33 @@
         return v if quad < near + quads else v * has_high
 
     guess = [kept(guess_s[quad], quad) for quad in range(total)]
+    applied = operated(guess)
     pre = [
-        kept(guess[quad] + scale * (source[quad] - operated(guess, quad)), quad)
-        for quad in range(total)
+        kept(guess[quad] + scale * (source[quad] - applied[quad]), quad) for quad in range(total)
     ]
+    applied = operated(pre)
     coarsest = [
-        kept(cell_mean(source[quad] - operated(pre, quad)), quad)
-        for quad in range(trim, total - trim)
+        kept(cell_mean(source[quad] - applied[quad]), quad) for quad in range(trim, total - trim)
     ]
     correction = [scale_b * v for v in coarsest]
     for sweep in range(NCOARSE - 1):
         last = sweep == NCOARSE - 2
         updated = []
+        turned = rolled(correction, 2)
         for quad in range(len(correction)):
             if last and quad in (0, len(correction) - 1):
                 updated.append(None)
                 continue
             c = correction[quad]
-            applied = screening * c - 0.25 * (beside(correction, quad, 2) - 6.0 * c)
+            applied = screening * c - 0.25 * (beside(correction, quad, 2, turned) - 6.0 * c)
             updated.append(kept(c + scale_b * (coarsest[quad] - applied), quad + trim))
         correction = updated
     start = near - 1
     found = [pre[quad] + correction[quad - trim] for quad in range(start, total - start)]
     for _ in range(NPOST):
+        applied = operated(found)
         found = [
-            kept(v + scale * (source[quad + start] - operated(found, quad)), quad + start)
+            kept(v + scale * (source[quad + start] - applied[quad]), quad + start)
             for quad, v in enumerate(found)
         ]
 
@@ -369,7 +395,7 @@
     )(own, core, chip)
 
 
-def finish_kernel(base_ref, wide_ref, rows_ref, *refs):
+def finish_kernel(inner_ref, outer_ref, wide_ref, rows_ref, *refs):
     edge_ref = refs[0] if len(refs) == 3 else None
     next_ref, potential_ref = refs[-2:]
     group, groups = lax.axis_index("grp"), lax.axis_size("grp")
@@ -400,16 +426,20 @@
                     term = term + down
                 if f == 3:
                     term = term + up
-                at = (4 * coarse + f, pl.ds(j, 32, stride=4), slice(None))
-                next_ref[at] = base_ref[at] + term
-
-
-def finish(base, wide, rows, edge, guess):
-    operands = [base, wide, rows] + ([] if edge is None else [edge])
+                plane, within = 4 * coarse + f, (pl.ds(j, 32, stride=4), slice(None))
+                if 2 <= plane < 6:
+                    base = inner_ref[(plane, *within)]
+                else:
+                    base = outer_ref[(plane % 4, *within)]
+                next_ref[(plane, *within)] = base + term
+
+
+def finish(inner, outer, wide, rows, edge, guess):
+    operands = [inner, outer, wide, rows] + ([] if edge is None else [edge])
     return pl.pallas_call(
         finish_kernel,
         out_shape=(
-            jax.ShapeDtypeStruct(base.shape, jnp.float32),
+            jax.ShapeDtypeStruct(inner.shape, jnp.float32),
             jax.ShapeDtypeStruct(guess.shape, jnp.float32),
         ),
         in_specs=[VMEM] * len(operands),
@@ -465,9 +495,10 @@
     if quads < HALO:
         edge = lax.ppermute(edge_of(bundle), both, edge_pairs(at, slabs, groups))
 
-    base = base_of(comp, first, second)
+    inner, chem = inner_of(comp)
     wide, rows = solve(bundle, core, chip, guess, edge is not None)
-    return finish(base, wide, rows, edge, guess)
+    outer = outer_of(comp, first, second, chem)
+    return finish(inner, outer, wide, rows, edge, guess)
 
 
 def idle_second(devices):

time: 19.6 us -> 19.9 us (1.015)
  waiting for transfers between devices: 3.43 us -> 3.64 us
  starting transfers between devices: 9.64 us -> 9.85 us
  local copies, waits for them, and re-layouts: 1.83 us -> 1.63 us
    ppermute x1, starting transfers between devices: 1.94 us -> 0.01 us  [per_device(): lax.ppermute(bundle, both, pairing(*((at(i, g), at(i + 1, g)) for i in ra...]
    ppermute x1, starting transfers between devices: 0.41 us -> 1.69 us  [per_device(): edge = lax.ppermute(edge_of(bundle), both, edge_pairs(at, slabs, groups))]
    ppermute x1, starting transfers between devices: 0.11 us -> 1.03 us  [per_device(): lax.ppermute(bundle, 'slab', pairing(*((i, i + 1) for i in range(0, slabs...]
    ppermute x3, waiting for transfers between devices: 1 us -> 1.9 us  [per_device(): block = lax.ppermute(message, 'grp', [(i, i ^ k) for i in range(groups)])]
    ppermute x1, waiting for transfers between devices: 2.42 us -> 1.72 us  [per_device(): lax.ppermute(bundle, both, pairing(*((at(i, g), at(i + 1, g)) for i in ra...]
    pallas_call x4 -> x5, Pallas kernels: 1.93 us -> 2.1 us  [the longest x1 0.92 us: finish(): pl.pallas_call(finish_kernel, out_shape=(jax.ShapeDtypeStruct(inner.shape...]
  transfers between devices with their start and end apart: 8 -> 8, of which waited for: 2 -> 2; matrix products, arithmetic and copies ran while one was open for 0% -> 0% of each run, Pallas kernels for 13% -> 14%
where the time goes in v1:
time: 19.9 us; the launch traced here: 19.7 us
  starting transfers between devices  9.85 us (49%)
  Pallas kernels  3.85 us (19%)
  waiting for transfers between devices  3.64 us (18%)
  local copies, waits for them, and re-layouts  1.63 us (8%)
  between operations  0.78 us (4%)
    ppermute x3, starting transfers between devices, per_device(): block = lax.ppermute(message, 'grp', [(i, i ^ k) for i in range(groups)])  4.51 us
    ppermute x1, starting transfers between devices, per_device(): lax.ppermute(first, both, pairing(*((d, d + 1) for d in range(0, devices,...  1.95 us
    ppermute x3, waiting for transfers between devices, per_device(): block = lax.ppermute(message, 'grp', [(i, i ^ k) for i in range(groups)])  1.9 us
    ppermute x1, waiting for transfers between devices, per_device(): lax.ppermute(bundle, both, pairing(*((at(i, g), at(i + 1, g)) for i in ra...  1.72 us
    ppermute x1, starting transfers between devices, per_device(): edge = lax.ppermute(edge_of(bundle), both, edge_pairs(at, slabs, groups))  1.69 us
    unnamed x6, local copies, waits for them, and re-layouts  1.6 us
    pallas_call x1, Pallas kernels, solve(): pl.pallas_call(functools.partial(solve_kernel, edged), out_shape=(jax.Sha...  1.36 us
    ppermute x1, starting transfers between devices, per_device(): lax.ppermute(bundle, 'slab', pairing(*((i, i + 1) for i in range(0, slabs...  1.03 us
  transfers between devices with their start and end apart: 8, of which 2 were waited for; matrix products, arithmetic and copies ran while one was open for 0% of the time, Pallas kernels for 14%

profile of v1, /device:TPU:0, one launch (start us, length us, event | category | flops | bytes accessed | tf_op | source)
XLA Modules:
  0.0 19.7 jit_solution(2866975215421189211)
XLA Ops:
  0.6 0.0 copy-start
  0.6 1.0 %copy-done = f32[8,128,128]{2,1,0:T(8,128)S(1)} copy-done((f32[8,128,128]{2,1,0:T(8,128)S(1)}, f32[8,128,128]{2,1,0:T(8,128)}, u32[]{:S(2)}) %copy-start) | copy-done | bytes 524312
  1.7 0.0 copy-start.2
  1.7 0.0 copy-start.1
  1.7 0.2 pool.1
  1.9 0.6 %copy-done.2 = f32[8,8,32]{2,1,0:T(8,128)S(1)} copy-done((f32[8,8,32]{2,1,0:T(8,128)S(1)}, f32[8,8,32]{2,1,0:T(8,128)}, u32[]{:S(2)}) %copy-start.2) | copy-done | bytes 8216
  2.4 0.1 pack.1
  2.5 3.0 %collective-permute-start.2 = (f32[32,128]{1,0:T(8,128)S(1)}, f32[32,128]{1,0:T(8,128)S(1)}, u32[]{:S(2)}, u32[]{:S(2)}) collective-permute-start(f32[32,128]{1,0:T(8,128)S(1)} %pack.1), channel_id=1, source_target_pairs={{0,1},{1,0},{2,3},{3,2},{4,5},{5,4},{6,7},{7,6},{8,9},{9,8},{10,11... | collective-permute-start | bytes 49160 | tf_op jit(solution)/shard_map/ppermute | solution.py:473
  5.5 1.5 %collective-permute-start.3 = (f32[32,128]{1,0:T(8,128)S(1)}, f32[32,128]{1,0:T(8,128)S(1)}, u32[]{:S(2)}, u32[]{:S(2)}) collective-permute-start(f32[32,128]{1,0:T(8,128)S(1)} %pack.1), channel_id=1, source_target_pairs={{0,2},{1,3},{2,0},{3,1},{4,6},{5,7},{6,4},{7,5},{8,10},{9,11},{10,... | collective-permute-start | bytes 49160 | tf_op jit(solution)/shard_map/ppermute | solution.py:473
  7.0 0.0 collective-permute-start.4
  7.0 1.9 %collective-permute-start = (f32[2,128,128]{2,1,0:T(8,128)S(1)}, f32[2,128,128]{2,1,0:T(8,128)S(1)}, u32[]{:S(2)}, u32[]{:S(2)}) collective-permute-start(f32[2,128,128]{2,1,0:T(8,128)S(1)} %get-tuple-element.10), channel_id=1, source_target_pairs={{0,1},{1,0},{2,3},{3,2},{4,5},{5,4},{6,7},{7,6},{8,9},{9,8},{10,11... | collective-permute-start | bytes 393224 | tf_op jit(solution)/shard_map/ppermute | solution.py:476
  9.0 0.7 %collective-permute-start.1 = (f32[2,128,128]{2,1,0:T(8,128)S(1)}, f32[2,128,128]{2,1,0:T(8,128)S(1)}, u32[]{:S(2)}, u32[]{:S(2)}) collective-permute-start(f32[2,128,128]{2,1,0:T(8,128)S(1)} %get-tuple-element.11), channel_id=1, source_target_pairs={{1,2},{2,1},{3,4},{4,3},{5,6},{6,5},{8,7},{7,8},{9,10},{10,9},{11,... | collective-permute-start | bytes 393224 | tf_op jit(solution)/shard_map/ppermute | solution.py:477
  9.7 0.0 collective-permute-done.2
  9.7 0.0 collective-permute-done.3
  9.7 1.9 %collective-permute-done.4 = f32[32,128]{1,0:T(8,128)S(1)} collective-permute-done((f32[32,128]{1,0:T(8,128)S(1)}, f32[32,128]{1,0:T(8,128)S(1)}, u32[]{:S(2)}, u32[]{:S(2)}) %collective-permute-start.4) | collective-permute-done | bytes 16416 | tf_op jit(solution)/shard_map/ppermute | solution.py:473
  11.6 1.0 %collective-permute-start.5 = (f32[4,32,128]{2,1,0:T(8,128)S(1)}, f32[4,32,128]{2,1,0:T(8,128)S(1)}, u32[]{:S(2)}, u32[]{:S(2)}) collective-permute-start(f32[4,32,128]{2,1,0:T(8,128)S(1)} %bitcast_dynamic-update-slice_fusion.own_ref), channel_id=1, source_target_pairs={{0,4},{4,0},{8,12},{12,8},{16,20},{20,16},{24,28},{28,24},{1,5},{5... | collective-permute-start | bytes 196616 | tf_op jit(solution)/shard_map/ppermute | solution.py:485
  12.7 0.0 collective-permute-start.6
  12.7 0.4 %edge.1 = f32[32,128]{1,0:T(8,128)S(1)} custom-call(f32[4,32,128]{2,1,0:T(8,128)S(1)} %bitcast_dynamic-update-slice_fusion.own_ref), custom_call_target="tpu_custom_call" | custom-call | flops 500000 | bytes 80000 | tf_op jit(solution)/shard_map/edge/pallas_call | solution.py:268
  13.1 1.7 %collective-permute-start.7 = (f32[32,128]{1,0:T(8,128)S(1)}, f32[32,128]{1,0:T(8,128)S(1)}, u32[]{:S(2)}, u32[]{:S(2)}) collective-permute-start(f32[32,128]{1,0:T(8,128)S(1)} %edge.1), channel_id=1, source_target_pairs={{3,8},{8,3},{12,7},{7,12},{16,11},{11,16},{20,15},{15,20},{19,24},... | collective-permute-start | bytes 49160 | tf_op jit(solution)/shard_map/ppermute | solution.py:496
  14.8 0.0 copy-done.1
  14.8 0.4 %inner.1 = (f32[8,128,128]{2,1,0:T(8,128)S(1)}, f32[8,128,128]{2,1,0:T(8,128)S(1)}) custom-call(f32[8,128,128]{2,1,0:T(8,128)S(1)} %copy-done.1), custom_call_target="tpu_custom_call" | custom-call | flops 3000000 | bytes 1500000 | tf_op jit(solution)/shard_map/inner/pallas_call | solution.py:133
  15.2 0.0 collective-permute-done.5.core_ref
  15.2 1.7 %collective-permute-done.6.chip_ref = f32[4,32,128]{2,1,0:T(8,128)S(1)} collective-permute-done((f32[4,32,128]{2,1,0:T(8,128)S(1)}, f32[4,32,128]{2,1,0:T(8,128)S(1)}, u32[]{:S(2)}, u32[]{:S(2)}) %collective-permute-start.6) | collective-permute-done | bytes 65568 | tf_op jit(solution)/shard_map/ppermute | solution.py:486
  16.9 1.4 %solve.1 = (f32[4,32,128]{2,1,0:T(8,128)S(1)}, f32[2,8,128]{2,1,0:T(8,128)S(1)}) custom-call(f32[4,32,128]{2,1,0:T(8,128)S(1)} %bitcast_dynamic-update-slice_fusion.own_ref, f32[4,32,128]{2,1,0:T(8,128)S(1)} %collective-permute-done.5.core_ref, f32[4,32,128]{2,1,0:T(8,128)S(1)} %collective-permute-done.6.chip_ref), custom_call_target="tpu_custom_call" | custom-call | flops 6000000 | bytes 500000 | tf_op jit(solution)/shard_map/solve/pallas_call | solution.py:380
  18.3 0.0 collective-permute-done.first_ref
  18.3 0.0 collective-permute-done.1.second_ref
  18.3 0.5 %outer.1.outer_ref = f32[4,128,128]{2,1,0:T(8,128)S(1)} custom-call(f32[8,128,128]{2,1,0:T(8,128)S(1)} %copy-done.1, f32[2,128,128]{2,1,0:T(8,128)S(1)} %collective-permute-done.first_ref, f32[2,128,128]{2,1,0:T(8,128)S(1)} %collective-permute-done.1.second_ref, f32[8,128,128]{2,1,0:T(8,128)S(1)} %get-tuple-element.12.chem_ref), custom_call_target="tpu_custom_call" | custom-call | flops 3000000 | bytes 1500000 | tf_op jit(solution)/shard_map/outer/pallas_call | solution.py:167
  18.8 0.0 collective-permute-done.7.refs_0_
  18.8 0.9 %finish.1 = (f32[8,128,128]{2,1,0:T(8,128)}, f32[8,8,32]{2,1,0:T(8,128)}) custom-call(f32[8,128,128]{2,1,0:T(8,128)S(1)} %get-tuple-element.9.inner_ref, f32[4,128,128]{2,1,0:T(8,128)S(1)} %outer.1.outer_ref, f32[4,32,128]{2,1,0:T(8,128)S(1)} %get-tuple-element.14.wide_ref, f32[2,8,128]{2,1,0:T(8,128)S(1)} %get-tuple-element.15.rows_ref, ...), custom_call_target="tpu_custom_call" | custom-call | flops 500000 | bytes 1100000 | tf_op jit(solution)/shard_map/finish/pallas_call | solution.py:439
  (5 shorter events, 0.0 us)
Async XLA Ops:
  0.6 1.0 %copy-start = (f32[8,128,128]{2,1,0:T(8,128)S(1)}, f32[8,128,128]{2,1,0:T(8,128)}, u32[]{:S(2)}) copy-start(f32[8,128,128]{2,1,0:T(8,128)} %comp_ref.5) | copy-start | bytes 1572868
  1.7 0.8 %copy-start.2 = (f32[8,8,32]{2,1,0:T(8,128)S(1)}, f32[8,8,32]{2,1,0:T(8,128)}, u32[]{:S(2)}) copy-start(f32[8,8,32]{2,1,0:T(8,128)} %guess_ref.1) | copy-start | bytes 24580
  1.7 13.1 %copy-start.1 = (f32[8,128,128]{2,1,0:T(8,128)S(1)}, f32[8,128,128]{2,1,0:T(8,128)}, u32[]{:S(2)}) copy-start(f32[8,128,128]{2,1,0:T(8,128)} %comp_ref.5) | copy-start | bytes 1572868
  2.5 7.2 %collective-permute-start.2 = (f32[32,128]{1,0:T(8,128)S(1)}, f32[32,128]{1,0:T(8,128)S(1)}, u32[]{:S(2)}, u32[]{:S(2)}) collective-permute-start(f32[32,128]{1,0:T(8,128)S(1)} %pack.1), channel_id=1, source_target_pairs={{0,1},{1,0},{2,3},{3,2},{4,5},{5,4},{6,7},{7,6},{8,9},{9,8},{10,11... | collective-permute-start | bytes 49160 | tf_op jit(solution)/shard_map/ppermute | solution.py:473
  5.5 4.2 %collective-permute-start.3 = (f32[32,128]{1,0:T(8,128)S(1)}, f32[32,128]{1,0:T(8,128)S(1)}, u32[]{:S(2)}, u32[]{:S(2)}) collective-permute-start(f32[32,128]{1,0:T(8,128)S(1)} %pack.1), channel_id=1, source_target_pairs={{0,2},{1,3},{2,0},{3,1},{4,6},{5,7},{6,4},{7,5},{8,10},{9,11},{10,... | collective-permute-start | bytes 49160 | tf_op jit(solution)/shard_map/ppermute | solution.py:473
  7.0 4.6 %collective-permute-start.4 = (f32[32,128]{1,0:T(8,128)S(1)}, f32[32,128]{1,0:T(8,128)S(1)}, u32[]{:S(2)}, u32[]{:S(2)}) collective-permute-start(f32[32,128]{1,0:T(8,128)S(1)} %pack.1), channel_id=1, source_target_pairs={{0,3},{1,2},{2,1},{3,0},{4,7},{5,6},{6,5},{7,4},{8,11},{9,10},{10,... | collective-permute-start | bytes 49160 | tf_op jit(solution)/shard_map/ppermute | solution.py:473
  7.0 11.3 %collective-permute-start = (f32[2,128,128]{2,1,0:T(8,128)S(1)}, f32[2,128,128]{2,1,0:T(8,128)S(1)}, u32[]{:S(2)}, u32[]{:S(2)}) collective-permute-start(f32[2,128,128]{2,1,0:T(8,128)S(1)} %get-tuple-element.10), channel_id=1, source_target_pairs={{0,1},{1,0},{2,3},{3,2},{4,5},{5,4},{6,7},{7,6},{8,9},{9,8},{10,11... | collective-permute-start | bytes 393224 | tf_op jit(solution)/shard_map/ppermute | solution.py:476
  9.0 9.3 %collective-permute-start.1 = (f32[2,128,128]{2,1,0:T(8,128)S(1)}, f32[2,128,128]{2,1,0:T(8,128)S(1)}, u32[]{:S(2)}, u32[]{:S(2)}) collective-permute-start(f32[2,128,128]{2,1,0:T(8,128)S(1)} %get-tuple-element.11), channel_id=1, source_target_pairs={{1,2},{2,1},{3,4},{4,3},{5,6},{6,5},{8,7},{7,8},{9,10},{10,9},{11,... | collective-permute-start | bytes 393224 | tf_op jit(solution)/shard_map/ppermute | solution.py:477
  11.6 3.6 %collective-permute-start.5 = (f32[4,32,128]{2,1,0:T(8,128)S(1)}, f32[4,32,128]{2,1,0:T(8,128)S(1)}, u32[]{:S(2)}, u32[]{:S(2)}) collective-permute-start(f32[4,32,128]{2,1,0:T(8,128)S(1)} %bitcast_dynamic-update-slice_fusion.own_ref), channel_id=1, source_target_pairs={{0,4},{4,0},{8,12},{12,8},{16,20},{20,16},{24,28},{28,24},{1,5},{5... | collective-permute-start | bytes 196616 | tf_op jit(solution)/shard_map/ppermute | solution.py:485
  12.7 4.3 %collective-permute-start.6 = (f32[4,32,128]{2,1,0:T(8,128)S(1)}, f32[4,32,128]{2,1,0:T(8,128)S(1)}, u32[]{:S(2)}, u32[]{:S(2)}) collective-permute-start(f32[4,32,128]{2,1,0:T(8,128)S(1)} %bitcast_dynamic-update-slice_fusion.own_ref), channel_id=1, source_target_pairs={{8,4},{4,8},{5,9},{9,5},{10,6},{6,10},{11,7},{7,11},{12,16},{16,12... | collective-permute-start | bytes 196616 | tf_op jit(solution)/shard_map/ppermute | solution.py:486
  13.1 5.7 %collective-permute-start.7 = (f32[32,128]{1,0:T(8,128)S(1)}, f32[32,128]{1,0:T(8,128)S(1)}, u32[]{:S(2)}, u32[]{:S(2)}) collective-permute-start(f32[32,128]{1,0:T(8,128)S(1)} %edge.1), channel_id=1, source_target_pairs={{3,8},{8,3},{12,7},{7,12},{16,11},{11,16},{20,15},{15,20},{19,24},... | collective-permute-start | bytes 49160 | tf_op jit(solution)/shard_map/ppermute | solution.py:496
